TPU v7x, 32 devices: a whole 2x2x4 slice. The times are simulated.
32 devices in a mesh: fsdp: 8 (over z, y), tp: 4 (over x, core).
Axes of the slice: x: 2, y: 2, z: 4, core: 2. Of those that a mesh axis runs over, the one named last changes fastest.
Arguments:
- base_o: bfloat16 [2, 8192, 8192], P(None, 'tp', 'fsdp'), may hold values from -0.0625 to 0.0625
- base_down: bfloat16 [2, 28672, 8192], P(None, 'tp', 'fsdp'), may hold values from -0.03125 to 0.03125
- factor_a_o: bfloat16 [2, 64, 4, 2048], P(None, None, None, 'fsdp'), may hold values from -0.0625 to 0.0625
- factor_b_o: bfloat16 [2, 8192, 64], P(None, 'fsdp'), may hold values from -1.1953125 to 1.1953125
- factor_a_down: bfloat16 [2, 64, 4, 7168], P(None, None, None, 'fsdp'), may hold values from -0.03125 to 0.03125
- factor_b_down: bfloat16 [2, 8192, 64], P(None, 'fsdp'), may hold values from -1.1953125 to 1.1953125
- magnitude_o: float32 [2, 8192], P(None, 'fsdp'), may hold values from 30 to 300
- magnitude_down: float32 [2, 8192], P(None, 'fsdp'), may hold values from 30 to 300
Outputs:
- merged_o: bfloat16 [2, 8192, 8192], P(None, 'tp', 'fsdp')
- merged_down: bfloat16 [2, 28672, 8192], P(None, 'tp', 'fsdp')
All inputs are finite; a program needn't handle non-finite values.
Results may differ from a plain program's by a relative error of at most 0.001.
Values may be sent and summed in bfloat16 or wider, within the bound.
A program may use at most 192 MiB of HBM per device.

v0:
```python
import jax
import jax.numpy as jnp
from jax import lax
from jax.sharding import PartitionSpec as P


def low_rank(rows_a, factor_b):
    return jnp.einsum("lri,lor->lio", rows_a, factor_b, preferred_element_type=jnp.float32)


def squares(base, delta):
    summed = base.astype(jnp.float32) + 0.25 * delta
    return (summed, jnp.sum(summed * summed, axis=1))


def finish(summed, square, magnitude):
    return (magnitude[:, None, :] * summed * lax.rsqrt(square + 1e-06)[:, None, :]).astype(
        jnp.bfloat16
    )


def local(
    base_o,
    base_down,
    factor_a_o,
    factor_b_o,
    factor_a_down,
    factor_b_down,
    magnitude_o,
    magnitude_down,
):
    column_t = lax.axis_index("tp")
    own_o = lax.dynamic_index_in_dim(factor_a_o, column_t, 2, keepdims=False)
    delta_o = low_rank(lax.all_gather(own_o, "fsdp", axis=2, tiled=True), factor_b_o)
    own_down = lax.dynamic_index_in_dim(factor_a_down, column_t, 2, keepdims=False)
    delta_down = low_rank(lax.all_gather(own_down, "fsdp", axis=2, tiled=True), factor_b_down)
    summed_o, partial_o = squares(base_o, delta_o)
    square_o = lax.psum(partial_o, "tp")
    merged_o = finish(summed_o, square_o, magnitude_o)
    summed_down, partial_down = squares(base_down, delta_down)
    square_down = lax.psum(partial_down, "tp")
    merged_down = finish(summed_down, square_down, magnitude_down)
    return (merged_o, merged_down)


def solution(mesh):
    return jax.shard_map(
        local,
        mesh=mesh,
        in_specs=(
            P(None, "tp", "fsdp"),
            P(None, "tp", "fsdp"),
            P(None, None, None, "fsdp"),
            P(None, "fsdp", None),
            P(None, None, None, "fsdp"),
            P(None, "fsdp", None),
            P(None, "fsdp"),
            P(None, "fsdp"),
        ),
        out_specs=(P(None, "tp", "fsdp"), P(None, "tp", "fsdp")),
        check_vma=False,
    )
```

profile of v0, /device:TPU:0, one launch (start us, length us, event | category | flops | bytes accessed | tf_op | source)
XLA Modules:
  0.0 159.7 jit_solution(17813612528903440651)
XLA Ops:
  7.2 0.0 copy-start
  7.2 0.0 copy-start.2
  7.2 0.0 all-gather.4.cloned.1.call-start
  7.2 1.1 copy-done
  8.4 0.5 constant_dynamic-slice_fusion
  8.8 0.7 copy.13
  9.5 0.0 all-gather.4.cloned.1.call-update
  9.6 1.1 constant_dynamic-slice_fusion.1
  10.7 33.7 %all-gather = bf16[2,64,1,2048]{3,1,0,2:T(8,128)(2,1)S(1)} all-gather(bf16[2,64,1,256]{3,1,0,2:T(8,128)(2,1)S(1)} %copy.12), channel_id=2, replica_groups=mesh['fsdp'=8,'tp'=4] {'fsdp'}, dimensions={3}, use_global_device_ids=true | all-gather | bytes 589824 | tf_op jit(solution)/shard_map/all_gather | solution.py:34
  44.4 10.1 %multiply_reduce_fusion.1 = (f32[2,1024]{1,0:T(2,128)S(1)}, f32[2,2048,1024]{2,1,0:T(8,128)}) fusion(bf16[2,2048,1024]{2,1,0:T(8,128)(2,1)} %param.8, bf16[2,1024,64]{1,2,0:T(8,128)(2,1)} %param.11, bf16[2,64,1,2048]{3,1,0,2:T(8,128)(2,1)S(1)} %all-gather), kind=kOutput, calls=%fused_computation.4 | convolution fusion | flops 557840384 | bytes 25960448 | tf_op jit(solution)/shard_map/lri,lor->lio/dot_general | solution.py:8
  54.5 0.0 copy-start.4
  54.5 7.0 %all-gather.4.cloned.1.call-done = bf16[2,64,1,7168]{3,1,0,2:T(8,128)(2,1)} async-done(((bf16[2,64,1,896]{3,1,0,2:T(8,128)(2,1)}), bf16[2,64,1,7168]{3,1,0,2:T(8,128)(2,1)}) %all-gather.4.cloned.1.call-update) | async-done | bytes 1835024 | tf_op jit(solution)/shard_map/all_gather | solution.py:36
  61.5 0.0 copy-done.2
  61.5 30.8 %multiply_reduce_fusion = (f32[2,1024]{1,0:T(2,128)S(1)}, f32[2,7168,1024]{2,1,0:T(8,128)}) fusion(bf16[2,7168,1024]{2,1,0:T(8,128)(2,1)} %param.9, bf16[2,1024,64]{1,2,0:T(8,128)(2,1)S(1)} %copy-done.2, bf16[2,64,1,7168]{3,1,0,2:T(8,128)(2,1)} %all-gather.4.cloned.1.call-done), kind=kOutput, calls=%fused_computation.1 | convolution fusion | flops 1952446464 | bytes 90185728 | tf_op jit(solution)/shard_map/lri,lor->lio/dot_general | solution.py:8
  92.3 10.1 %all-reduce = (f32[2,1024]{1,0:T(2,128)S(1)}, f32[2,1024]{1,0:T(2,128)S(1)}) all-reduce(f32[2,1024]{1,0:T(2,128)S(1)} %get-tuple-element.4, f32[2,1024]{1,0:T(2,128)S(1)} %get-tuple-element.6), channel_id=1, replica_groups=mesh['fsdp'=8,'tp'=4] {'tp'}, use_global_device_ids=true, to_apply=%region_1.2 | all-reduce | flops 4096 | bytes 32768 | tf_op jit(solution)/shard_map/psum | solution.py:38
  102.5 0.0 copy-done.4
  102.5 0.0 copy-start.3
  102.5 12.2 %multiply_convert_fusion.1 = bf16[2,2048,1024]{2,1,0:T(8,128)(2,1)} fusion(f32[2,2048,1024]{2,1,0:T(8,128)} %get-tuple-element.5, bf16[2,2048,1024]{2,1,0:T(8,128)(2,1)} %param.8, f32[2,1024]{1,0:T(2,128)S(1)} %get-tuple-element.9, f32[2,1024]{1,0:T(2,128)S(1)} %copy-done.4), kind=kLoop, calls=%fused_computation.3 | loop fusion | flops 25165824 | bytes 33570816 | tf_op jit(solution)/shard_map/convert_element_type | solution.py:17
  114.7 0.0 copy-done.3
  114.7 0.0 copy-start.1
  114.7 38.2 %multiply_convert_fusion = bf16[2,7168,1024]{2,1,0:T(8,128)(2,1)} fusion(f32[2,7168,1024]{2,1,0:T(8,128)} %get-tuple-element.7, bf16[2,7168,1024]{2,1,0:T(8,128)(2,1)} %param.9, f32[2,1024]{1,0:T(2,128)S(1)} %get-tuple-element.8, f32[2,1024]{1,0:T(2,128)S(1)} %copy-done.3), kind=kLoop, calls=%fused_computation | loop fusion | flops 88080384 | bytes 117456896 | tf_op jit(solution)/shard_map/convert_element_type | solution.py:17
  152.8 0.0 copy-done.1
  (2 shorter events, 0.0 us)
Async XLA Ops:
  7.2 1.2 copy-start
  7.2 54.3 %copy-start.2 = (bf16[2,1024,64]{1,2,0:T(8,128)(2,1)S(1)}, bf16[2,1024,64]{1,2,0:T(8,128)(2,1)}, u32[]{:S(2)}) copy-start(bf16[2,1024,64]{1,2,0:T(8,128)(2,1)} %param.13) | copy-start | bytes 786436
  7.2 54.3 %all-gather.4.cloned.1.call-start = ((), (), s32[]{:S(2)}) async-start(), calls=%async_computation | async-start | bytes 2064384 | tf_op jit(solution)/shard_map/all_gather | solution.py:36
  54.5 48.0 %copy-start.4 = (f32[2,1024]{1,0:T(2,128)S(1)}, f32[2,1024]{1,0:T(2,128)}, u32[]{:S(2)}) copy-start(f32[2,1024]{1,0:T(2,128)} %param.14) | copy-start | bytes 24580
  102.5 12.2 %copy-start.3 = (f32[2,1024]{1,0:T(2,128)S(1)}, f32[2,1024]{1,0:T(2,128)}, u32[]{:S(2)}) copy-start(f32[2,1024]{1,0:T(2,128)} %param.15) | copy-start | bytes 24580
  114.7 38.2 %copy-start.1 = (bf16[2,64,4,896]{3,2,1,0:T(4,128)(2,1)S(1)}, bf16[2,64,4,896]{3,2,1,0:T(4,128)(2,1)}, u32[]{:S(2)}) copy-start(bf16[2,64,4,896]{3,2,1,0:T(4,128)(2,1)} %param.12) | copy-start | bytes 2752516
Sparse Core Ops, SparseCore 0:
  10.8 50.6 all-gather.3
where the time goes:
time: 160 us
  other arithmetic  50.4 us (32%)
  blocking collectives  43.8 us (27%)
  matrix products  40.9 us (26%)
  between operations  14.1 us (9%)
  waiting for transfers between devices  7.03 us (4%)
  local copies, waits for them, and re-layouts  3.44 us (2%)
    convert_element_type x2, other arithmetic, finish(): (magnitude[:, None, :] * summed * lax.rsqrt(square + 1e-06)[:, None, :])....  50.4 us
    dot_general x2, matrix products, low_rank(): jnp.einsum('lri,lor->lio', rows_a, factor_b, preferred_element_type=jnp.f...  40.9 us
    all_gather x1, blocking collectives, local(): lax.all_gather(own_o, 'fsdp', axis=2, tiled=True)  33.7 us
    psum x1, blocking collectives, local(): square_o = lax.psum(partial_o, 'tp')  10.1 us
    all_gather x1, waiting for transfers between devices, local(): lax.all_gather(own_down, 'fsdp', axis=2, tiled=True)  7.01 us
  transfers between devices with their start and end apart: 1, of which 1 were waited for; matrix products, arithmetic and copies ran while one was open for 7% of the time, Pallas kernels for 0%

commit v1 on v0

--- a/solution.py
+++ b/solution.py
@@ -35,7 +35,7 @@
     own_down = lax.dynamic_index_in_dim(factor_a_down, column_t, 2, keepdims=False)
     delta_down = low_rank(lax.all_gather(own_down, "fsdp", axis=2, tiled=True), factor_b_down)
     summed_o, partial_o = squares(base_o, delta_o)
-    square_o = lax.psum(partial_o, "tp")
+    square_o = jnp.sum(lax.all_gather(partial_o, "tp"), axis=0)
     merged_o = finish(summed_o, square_o, magnitude_o)
     summed_down, partial_down = squares(base_down, delta_down)
     square_down = lax.psum(partial_down, "tp")

time: 160 us -> 155 us (0.969)
  waiting for transfers between devices: 7.03 us -> 0.02 us
  blocking collectives: 43.8 us -> 46.1 us
    all_gather x1, waiting for transfers between devices: 7.01 us -> 0.01 us  [local(): lax.all_gather(own_down, 'fsdp', axis=2, tiled=True)]
    all_gather x0 -> x1, blocking collectives: none -> 5.17 us  [local(): square_o = jnp.sum(lax.all_gather(partial_o, 'tp'), axis=0)]
    psum x1, blocking collectives: 10.1 us -> 6.99 us  [local(): square_down = lax.psum(partial_down, 'tp')]
  transfers between devices with their start and end apart: 1 -> 1, of which waited for: 1 -> 0; matrix products, arithmetic and copies ran while one was open for 7% -> 15% of each run, Pallas kernels for 0% -> 0%
where the time goes in v1:
time: 155 us
  other arithmetic  50.5 us (33%)
  blocking collectives  46.1 us (30%)
  matrix products  40.9 us (26%)
  between operations  14.1 us (9%)
  local copies, waits for them, and re-layouts  3.43 us (2%)
    convert_element_type x2, other arithmetic, finish(): (magnitude[:, None, :] * summed * lax.rsqrt(square + 1e-06)[:, None, :])....  50.4 us
    dot_general x2, matrix products, low_rank(): jnp.einsum('lri,lor->lio', rows_a, factor_b, preferred_element_type=jnp.f...  40.9 us
    all_gather x1, blocking collectives, local(): lax.all_gather(own_o, 'fsdp', axis=2, tiled=True)  33.9 us
    psum x1, blocking collectives, local(): square_down = lax.psum(partial_down, 'tp')  6.99 us
    all_gather x1, blocking collectives, local(): square_o = jnp.sum(lax.all_gather(partial_o, 'tp'), axis=0)  5.17 us
  transfers between devices with their start and end apart: 1, of which 0 were waited for; matrix products, arithmetic and copies ran while one was open for 15% of the time, Pallas kernels for 0%

profile of v1, /device:TPU:0, one launch (start us, length us, event | category | flops | bytes accessed | tf_op | source)
XLA Modules:
  0.0 155.1 jit_solution(5781365325209540300)
XLA Ops:
  7.2 0.0 copy-start
  7.2 0.0 copy-start.4
  7.2 0.0 all-gather.6.cloned.1.call-start
  7.2 1.1 copy-done
  8.4 0.5 constant_dynamic-slice_fusion
  8.8 0.7 copy.15
  9.5 0.0 all-gather.6.cloned.1.call-update
  9.6 1.1 constant_dynamic-slice_fusion.1
  10.7 33.9 %all-gather = bf16[2,64,1,2048]{3,1,0,2:T(8,128)(2,1)S(1)} all-gather(bf16[2,64,1,256]{3,1,0,2:T(8,128)(2,1)S(1)} %copy.14), channel_id=2, replica_groups=mesh['fsdp'=8,'tp'=4] {'fsdp'}, dimensions={3}, use_global_device_ids=true | all-gather | bytes 589824 | tf_op jit(solution)/shard_map/all_gather | solution.py:34
  44.6 10.1 %multiply_reduce_fusion.1 = (f32[2,1024]{1,0:T(2,128)S(1)}, f32[2,2048,1024]{2,1,0:T(8,128)}) fusion(bf16[2,2048,1024]{2,1,0:T(8,128)(2,1)} %param.8, bf16[2,1024,64]{1,2,0:T(8,128)(2,1)} %param.11, bf16[2,64,1,2048]{3,1,0,2:T(8,128)(2,1)S(1)} %all-gather), kind=kOutput, calls=%fused_computation.4 | convolution fusion | flops 557840384 | bytes 25960448 | tf_op jit(solution)/shard_map/lri,lor->lio/dot_general | solution.py:8
  54.7 5.2 %all-gather.3 = f32[4,2,1024]{2,1,0:T(2,128)S(1)} all-gather(f32[1,2,1024]{2,1,0:T(2,128)S(1)} %bitcast.13), channel_id=3, replica_groups=mesh['fsdp'=8,'tp'=4] {'tp'}, dimensions={0}, use_global_device_ids=true | all-gather | bytes 40960 | tf_op jit(solution)/shard_map/all_gather | solution.py:38
  59.9 0.0 copy-done.4
  59.9 0.0 copy-start.2
  59.9 12.2 %multiply_convert_fusion.1 = bf16[2,2048,1024]{2,1,0:T(8,128)(2,1)} fusion(f32[2,2048,1024]{2,1,0:T(8,128)} %get-tuple-element.3, bf16[2,2048,1024]{2,1,0:T(8,128)(2,1)} %param.8, f32[2,1024]{1,0:T(2,128)S(1)} %add_rsqrt_fusion.1, f32[2,1024]{1,0:T(2,128)S(1)} %copy-done.4), kind=kLoop, calls=%fused_computation.3 | loop fusion | flops 25165824 | bytes 33570816 | tf_op jit(solution)/shard_map/convert_element_type | solution.py:17
  72.1 0.0 copy-start.3
  72.1 0.0 all-gather.6.cloned.1.call-done
  72.1 0.0 copy-done.2
  72.1 30.8 %multiply_reduce_fusion = (f32[2,1024]{1,0:T(2,128)S(1)}, f32[2,7168,1024]{2,1,0:T(8,128)}) fusion(bf16[2,7168,1024]{2,1,0:T(8,128)(2,1)} %param.9, bf16[2,1024,64]{1,2,0:T(8,128)(2,1)S(1)} %copy-done.2, bf16[2,64,1,7168]{3,1,0,2:T(8,128)(2,1)} %all-gather.6.cloned.1.call-done), kind=kOutput, calls=%fused_computation.1 | convolution fusion | flops 1952446464 | bytes 90185728 | tf_op jit(solution)/shard_map/lri,lor->lio/dot_general | solution.py:8
  103.0 7.0 %psum.7 = f32[2,1024]{1,0:T(2,128)S(1)} all-reduce(f32[2,1024]{1,0:T(2,128)S(1)} %get-tuple-element.4), channel_id=1, replica_groups=mesh['fsdp'=8,'tp'=4] {'tp'}, use_global_device_ids=true, to_apply=%region_3.4 | all-reduce | flops 2048 | bytes 16384 | tf_op jit(solution)/shard_map/psum | solution.py:41
  110.0 0.0 copy-done.3
  110.0 0.0 copy-start.1
  110.0 38.2 %multiply_convert_fusion = bf16[2,7168,1024]{2,1,0:T(8,128)(2,1)} fusion(f32[2,7168,1024]{2,1,0:T(8,128)} %get-tuple-element.5, bf16[2,7168,1024]{2,1,0:T(8,128)(2,1)} %param.9, f32[2,1024]{1,0:T(2,128)S(1)} %add_rsqrt_fusion, f32[2,1024]{1,0:T(2,128)S(1)} %copy-done.3), kind=kLoop, calls=%fused_computation | loop fusion | flops 88080384 | bytes 117456896 | tf_op jit(solution)/shard_map/convert_element_type | solution.py:17
  148.2 0.0 copy-done.1
  (4 shorter events, 0.1 us)
Async XLA Ops:
  7.2 1.2 copy-start
  7.2 52.7 %copy-start.4 = (f32[2,1024]{1,0:T(2,128)S(1)}, f32[2,1024]{1,0:T(2,128)}, u32[]{:S(2)}) copy-start(f32[2,1024]{1,0:T(2,128)} %param.14) | copy-start | bytes 24580
  7.2 65.0 %all-gather.6.cloned.1.call-start = ((), (), s32[]{:S(2)}) async-start(), calls=%async_computation | async-start | bytes 2064384 | tf_op jit(solution)/shard_map/all_gather | solution.py:36
  59.9 12.2 %copy-start.2 = (bf16[2,1024,64]{1,2,0:T(8,128)(2,1)S(1)}, bf16[2,1024,64]{1,2,0:T(8,128)(2,1)}, u32[]{:S(2)}) copy-start(bf16[2,1024,64]{1,2,0:T(8,128)(2,1)} %param.13) | copy-start | bytes 786436
  72.1 37.9 %copy-start.3 = (f32[2,1024]{1,0:T(2,128)S(1)}, f32[2,1024]{1,0:T(2,128)}, u32[]{:S(2)}) copy-start(f32[2,1024]{1,0:T(2,128)} %param.15) | copy-start | bytes 24580
  110.0 38.2 %copy-start.1 = (bf16[2,64,4,896]{3,2,1,0:T(4,128)(2,1)S(1)}, bf16[2,64,4,896]{3,2,1,0:T(4,128)(2,1)}, u32[]{:S(2)}) copy-start(bf16[2,64,4,896]{3,2,1,0:T(4,128)(2,1)} %param.12) | copy-start | bytes 2752516
Sparse Core Ops, SparseCore 0:
  10.2 50.2 all-gather.5
